TPU v7x, 256 devices: a whole 4x4x8 slice. The times are simulated.
256 devices in a mesh: dp: 8 (over y, core), tensor: 32 (over z, x).
Axes of the slice: x: 4, y: 4, z: 8, core: 2. Of those that a mesh axis runs over, the one named last changes fastest.
Arguments:
- hidden: bfloat16 [1280, 16384], P(None, ('dp', 'tensor')), may hold values from -100 to 100
- gain: bfloat16 [1, 16384], P(None, ('dp', 'tensor')), may hold values from 0.5 to 2, as said below
- head_weight: bfloat16 [16384, 65536], P('dp', 'tensor'), may hold values from -3 to 3
- draft_probs: float32 [1280, 65536], P(('dp', 'tensor')), may hold values from 0 to 1, as said below
- draft_ids: int32 [1280], P('dp'), may hold values from 0 to 65535
- reject_at: int32 [256], P('dp'), may hold values from 0 to 4
Outputs:
- token_logprob: float32 [1280], P('dp')
- residual: float32 [256, 65536], P('dp', 'tensor')
Inputs may be any that keep to these rules, and one draw needn't show every extreme that they name: `draft_probs`: every row is a probability distribution over the 65536 entries that sums to one. `gain`: positive.
All inputs are finite; a program needn't handle non-finite values.
Results may differ from a plain program's by a relative error of at most 0.0005.
The roundings to bfloat16 on the way count: a program that leaves them out, or rounds other values in their place, can miss the bound.
Values may be sent and summed in bfloat16 or wider, within the bound.
A program may use at most 128 MiB of HBM per device.

v0:
```python
import jax
import jax.numpy as jnp
from jax import lax
from jax.sharding import Mesh
from jax.sharding import PartitionSpec as P

D = 16384
VOCAB = 65536
POS = 5
TENSOR = ("tensor_0", "tensor_1")
DP_TENSOR = ("dp", "tensor_0", "tensor_1")
EPS = 1e-05


def gather_turned(arrays, axis, dims):
    turned = [jnp.moveaxis(a, dim, 0) for a, dim in zip(arrays, dims)]
    widths = [t[0].size for t in turned]
    both = jnp.concatenate([t.reshape(-1, w) for t, w in zip(turned, widths)], axis=1)
    out = lax.all_gather(both, axis, axis=0, tiled=True)
    tiles = jnp.split(out, [sum(widths[:k]) for k in range(1, len(widths))], axis=1)
    return tuple(
        (
            jnp.moveaxis(b.reshape(-1, *t.shape[1:]), 0, dim)
            for b, t, dim in zip(tiles, turned, dims)
        )
    )


def sent_to_all(shard, axis):
    devices = lax.axis_size(axis)
    return lax.all_to_all(
        jnp.broadcast_to(shard[None], (devices, *shard.shape)), axis, 0, 0, tiled=True
    )


def of_everyone(shard, axis):
    everything = sent_to_all(shard, axis)
    return jnp.sum(everything, axis=0)


def collected_together(shard, axis):
    leaves = jax.tree.leaves(shard)
    order = sorted(range(len(leaves)), key=lambda k: -leaves[k].size)
    width = (1, *leaves[order[0]].shape)[-1]
    lines = [
        jnp.pad(leaves[k].reshape(-1), (0, -leaves[k].size % width)).reshape(-1, width)
        for k in order
    ]
    both, at, found = (sent_to_all(jnp.concatenate(lines), axis), 0, {})
    for k, line in zip(order, lines):
        share = both[:, at : at + len(line)].reshape(len(both), -1)
        found[k] = share[:, : leaves[k].size].reshape(-1, *leaves[k].shape)
        at += len(line)
    numbers = iter(range(len(leaves)))
    return jax.tree.map(lambda _: found[next(numbers)], shard)


def combined_pairwise(pieces, combine):
    while len(jax.tree.leaves(pieces)[0]) > 1:
        pieces = jax.vmap(combine)(
            *(jax.tree.map(lambda part: part[side::2], pieces) for side in (0, 1))
        )
    return jax.tree.map(lambda part: part[0], pieces)


def merged(shard, axis, combine):
    pieces = collected_together(shard, axis)
    return combined_pairwise(pieces, combine)


def in_blocks(shard, dim, devices):
    before, after = (shard.shape[:dim], shard.shape[dim + 1 :])
    return jnp.moveaxis(shard.reshape(*before, devices, -1, *after), dim, 0)


def laid_out(tiles, dim):
    tiles = jnp.moveaxis(tiles, 0, dim)
    shape = tiles.shape
    return tiles.reshape(*shape[:dim], shape[dim] * shape[dim + 1], *shape[dim + 2 :])


def exchange_in_order(tiles, axes, order):
    inside = tiles.shape[1:]
    out = tiles.reshape(*(lax.axis_size(a) for a in axes), *inside)
    for k in order:
        out = lax.all_to_all(out, axes[k], k, k, tiled=True)
    return out.reshape(-1, *inside)


def stepwise_exchange(shard, axes, order, split_dim, concat_dim):
    tiles = in_blocks(shard, split_dim, lax.axis_size(axes))
    return laid_out(exchange_in_order(tiles, axes, order), concat_dim)


def combine_stats(first, second):
    top = jnp.maximum(first[0], second[0])
    total = first[1] * jnp.exp(first[0] - top) + second[1] * jnp.exp(second[0] - top)
    return (top, total, first[2] + second[2])


def shards(hidden, gain, head_weight, draft_probs, draft_ids, reject_at):
    raw, gains = gather_turned((hidden, gain), TENSOR, (1, 1))
    values = raw.astype(jnp.float32)
    squares = of_everyone(jnp.sum(values * values, axis=1), "dp")
    normed = (values * lax.rsqrt(squares / D + EPS)[:, None] * gains.astype(jnp.float32)).astype(
        jnp.bfloat16
    )
    logits = lax.psum_scatter(
        jnp.dot(normed, head_weight, preferred_element_type=jnp.float32),
        "dp",
        scatter_dimension=0,
        tiled=True,
    )
    width = logits.shape[1]
    columns = lax.broadcasted_iota(jnp.int32, (1, width), 1) + lax.axis_index(TENSOR) * width
    local_max = jnp.max(logits, axis=1)
    local_pick = jnp.sum(jnp.where(columns == draft_ids[:, None], logits, 0.0), axis=1)
    local_total = jnp.sum(jnp.exp(logits - local_max[:, None]), axis=1)
    top, total, picked = merged((local_max, local_total, local_pick), TENSOR, combine_stats)
    logz = top + jnp.log(total)
    token_logprob = picked - logz
    requests = reject_at.shape[0]
    where_at = reject_at[:, None, None]
    chosen = jnp.take_along_axis(logits.reshape(requests, POS, width), where_at, axis=1)[:, 0]
    chosen_logz = jnp.take_along_axis(logz.reshape(requests, POS), reject_at[:, None], axis=1)[:, 0]
    owned = draft_probs.shape[0] // POS
    mine = lax.dynamic_slice_in_dim(reject_at, lax.axis_index(TENSOR) * owned, owned, 0)
    local_rows = jnp.take_along_axis(
        draft_probs.reshape(owned, POS, draft_probs.shape[1]), mine[:, None, None], axis=1
    )[:, 0]
    drafts = stepwise_exchange(local_rows, TENSOR, (0, 1), 1, 0)
    target = jnp.exp(chosen - chosen_logz[:, None])
    kept = jnp.maximum(target - drafts, 0.0)
    mass = of_everyone(jnp.sum(kept, axis=1), TENSOR)
    residual = VOCAB * kept / mass[:, None]
    return (token_logprob, residual)


def solution(mesh):
    finer = Mesh(mesh.devices.reshape(mesh.shape["dp"], 8, 4), ("dp", "tensor_0", "tensor_1"))
    return jax.shard_map(
        shards,
        mesh=finer,
        in_specs=(
            P(None, DP_TENSOR),
            P(None, DP_TENSOR),
            P("dp", TENSOR),
            P(DP_TENSOR, None),
            P("dp"),
            P("dp"),
        ),
        out_specs=(P("dp"), P("dp", TENSOR)),
        check_vma=False,
    )
```

profile of v0, /device:TPU:2, one launch (start us, length us, event | category | flops | bytes accessed | tf_op | source)
XLA Modules:
  0.0 244.7 jit_solution(11810999547633045622)
XLA Ops:
  7.2 0.8 copy.43
  8.0 1.6 pad_maximum_fusion
  9.6 89.8 %all-gather.2.cloned.1.call-done = bf16[2048,1281]{1,0:T(8,128)(2,1)} async-done(((bf16[64,1281]{1,0:T(8,128)(2,1)}), bf16[2048,1281]{1,0:T(8,128)(2,1)}) %all-gather.2.cloned.1.call-update) | async-done | bytes 5246992 | tf_op jit(solution)/shard_map/all_gather | solution.py:19
  99.4 3.6 %fusion = f32[1280]{0:T(1024)S(1)} fusion(bf16[2048,1281]{1,0:T(8,128)(2,1)} %all-gather.2.cloned.1.call-done), kind=kLoop, calls=%fused_computation.4 | loop fusion | flops 7863040 | bytes 5248000 | tf_op jit(solution)/shard_map/reduce_sum | solution.py:104
  103.0 0.6 broadcast_in_dim.59
  103.6 4.3 %all-to-all-start = ((f32[8,1,1280]{2,1,0:T(1,128)}), f32[8,1,1280]{2,1,0:T(1,128)S(1)}, u32[]{:S(2)}, u32[]{:S(2)}) async-start(f32[8,1,1280]{2,1,0:T(1,128)} %broadcast_in_dim.59), calls=%async_computation | async-start | bytes 81920 | tf_op jit(solution)/shard_map/all_to_all | solution.py:31
  108.0 1.3 convert_reduce_fusion
  109.2 4.2 %all-to-all-done = f32[8,1,1280]{2,1,0:T(1,128)S(1)} async-done(((f32[8,1,1280]{2,1,0:T(1,128)}), f32[8,1,1280]{2,1,0:T(1,128)S(1)}, u32[]{:S(2)}, u32[]{:S(2)}) %all-to-all-start) | async-done | bytes 40992 | tf_op jit(solution)/shard_map/all_to_all | solution.py:31
  113.5 17.9 %fusion.3 = f32[1280,2048]{1,0:T(8,128)} fusion(bf16[2048,2048]{1,0:T(8,128)(2,1)} %param.8, f32[2048]{0:T(1024)S(1)} %convert_reduce_fusion, f32[1280]{0:T(1024)S(1)} %add_rsqrt_fusion, bf16[2048,1281]{1,0:T(8,128)(2,1)} %all-gather.2.cloned.1.call-done), kind=kOutput, calls=%fused_computation.7 | convolution fusion | flops 10747904000 | bytes 24130560 | tf_op jit(solution)/shard_map/dot_general | solution.py:109
  134.5 2.4 fusion.8
  136.9 0.8 select_n.68
  137.7 4.0 %all-to-all-start.2 = ((f32[8,4,1,2048]{3,1,2,0:T(4,128)}), f32[8,4,1,2048]{3,1,2,0:T(4,128)S(1)}, u32[]{:S(2)}, u32[]{:S(2)}) async-start(f32[8,4,1,2048]{3,1,2,0:T(4,128)} %select_n.68), calls=%async_computation.3 | async-start | bytes 524288 | tf_op jit(solution)/shard_map/all_to_all | solution.py:86
  141.8 11.8 %all-to-all-done.2 = f32[8,4,1,2048]{3,1,2,0:T(4,128)S(1)} async-done(((f32[8,4,1,2048]{3,1,2,0:T(4,128)}), f32[8,4,1,2048]{3,1,2,0:T(4,128)S(1)}, u32[]{:S(2)}, u32[]{:S(2)}) %all-to-all-start.2) | async-done | bytes 262176 | tf_op jit(solution)/shard_map/all_to_all | solution.py:86
  153.5 0.9 copy.48
  154.4 5.2 %all-to-all-start.3 = ((f32[8,4,1,2048]{3,0,2,1:T(8,128)}), f32[8,4,1,2048]{3,0,2,1:T(8,128)S(1)}, u32[]{:S(2)}, u32[]{:S(2)}) async-start(f32[8,4,1,2048]{3,0,2,1:T(8,128)} %copy.48), calls=%async_computation.4 | async-start | bytes 524288 | tf_op jit(solution)/shard_map/all_to_all | solution.py:86
  159.6 33.1 %reduce-scatter.2.cloned.1.call-done = f32[160,2048]{1,0:T(8,128)} async-done(((f32[1280,2048]{1,0:T(8,128)}), f32[160,2048]{1,0:T(8,128)}) %reduce-scatter.2.cloned.1.call-update) | async-done | bytes 1310736 | tf_op jit(solution)/shard_map/reduce_scatter | solution.py:108
  192.7 1.5 reduce_max.9
  194.1 1.8 exponential_reduce_fusion
  196.0 0.8 reshape.248
  196.8 10.2 %all-to-all-start.1 = ((f32[32,1,480]{2,1,0:T(1,128)}), f32[32,1,480]{2,1,0:T(1,128)S(1)}, u32[]{:S(2)}, u32[]{:S(2)}) async-start(f32[32,1,480]{2,1,0:T(1,128)} %reshape.248), calls=%async_computation.2 | async-start | bytes 131072 | tf_op jit(solution)/shard_map/all_to_all | solution.py:31
  207.2 0.8 reshape_reshape.3
  208.0 1.5 reshape.176
  209.4 0.8 copy.47
  210.2 0.9 gather_fusion
  211.1 4.5 %all-to-all-done.1 = f32[32,1,480]{2,1,0:T(1,128)S(1)} async-done(((f32[32,1,480]{2,1,0:T(1,128)}), f32[32,1,480]{2,1,0:T(1,128)S(1)}, u32[]{:S(2)}, u32[]{:S(2)}) %all-to-all-start.1) | async-done | bytes 61472 | tf_op jit(solution)/shard_map/all_to_all | solution.py:31
  216.2 0.8 reduce.15
  218.3 0.7 fusion.18
  219.1 0.7 gather_fusion.1
  220.2 1.2 fusion.13
  222.2 5.3 %all-to-all-start.4 = ((f32[32,1,32]{2,1,0:T(1,128)}), f32[32,1,32]{2,1,0:T(1,128)S(1)}, u32[]{:S(2)}, u32[]{:S(2)}) async-start(f32[32,1,32]{2,1,0:T(1,128)} %broadcast_in_dim.72), calls=%async_computation.5 | async-start | bytes 32768 | tf_op jit(solution)/shard_map/all_to_all | solution.py:31
  228.1 8.0 %all-to-all-done.4 = f32[32,1,32]{2,1,0:T(1,128)S(1)} async-done(((f32[32,1,32]{2,1,0:T(1,128)}), f32[32,1,32]{2,1,0:T(1,128)S(1)}, u32[]{:S(2)}, u32[]{:S(2)}) %all-to-all-start.4) | async-done | bytes 4128 | tf_op jit(solution)/shard_map/all_to_all | solution.py:31
  236.1 1.8 multiply_divide_fusion
  (72 shorter events, 5.3 us)
Async XLA Ops:
  7.2 92.2 %all-gather.2.cloned.1.call-start = ((), (), s32[]{:S(2)}) async-start(), calls=%async_computation.6 | async-start | bytes 5947392 | tf_op jit(solution)/shard_map/all_gather | solution.py:19
  103.6 9.8 %all-to-all-start = ((f32[8,1,1280]{2,1,0:T(1,128)}), f32[8,1,1280]{2,1,0:T(1,128)S(1)}, u32[]{:S(2)}, u32[]{:S(2)}) async-start(f32[8,1,1280]{2,1,0:T(1,128)} %broadcast_in_dim.59), calls=%async_computation | async-start | bytes 81920 | tf_op jit(solution)/shard_map/all_to_all | solution.py:31
  107.9 84.8 %reduce-scatter.2.cloned.1.call-start = ((), (), s32[]{:S(2)}) async-start(), calls=%async_computation.7 | async-start | bytes 11796480 | tf_op jit(solution)/shard_map/reduce_scatter | solution.py:108
  131.3 0.7 copy-start.2
  131.3 62.8 %copy-start.1 = (s32[160]{0:T(256)S(1)}, s32[160]{0:T(256)}, u32[]{:S(2)}) copy-start(s32[160]{0:T(256)} %param.10) | copy-start | bytes 1924
  137.7 15.8 %all-to-all-start.2 = ((f32[8,4,1,2048]{3,1,2,0:T(4,128)}), f32[8,4,1,2048]{3,1,2,0:T(4,128)S(1)}, u32[]{:S(2)}, u32[]{:S(2)}) async-start(f32[8,4,1,2048]{3,1,2,0:T(4,128)} %select_n.68), calls=%async_computation.3 | async-start | bytes 524288 | tf_op jit(solution)/shard_map/all_to_all | solution.py:86
  154.4 42.4 %all-to-all-start.3 = ((f32[8,4,1,2048]{3,0,2,1:T(8,128)}), f32[8,4,1,2048]{3,0,2,1:T(8,128)S(1)}, u32[]{:S(2)}, u32[]{:S(2)}) async-start(f32[8,4,1,2048]{3,0,2,1:T(8,128)} %copy.48), calls=%async_computation.4 | async-start | bytes 524288 | tf_op jit(solution)/shard_map/all_to_all | solution.py:86
  196.8 10.4 %copy-start = (f32[8,4,1,2048]{3,0,2,1:T(8,128)}, f32[8,4,1,2048]{3,0,2,1:T(8,128)S(1)}, u32[]{:S(2)}) copy-start(f32[8,4,1,2048]{3,0,2,1:T(8,128)S(1)} %all-to-all-done.3) | copy-start | bytes 786436
  196.8 18.8 %all-to-all-start.1 = ((f32[32,1,480]{2,1,0:T(1,128)}), f32[32,1,480]{2,1,0:T(1,128)S(1)}, u32[]{:S(2)}, u32[]{:S(2)}) async-start(f32[32,1,480]{2,1,0:T(1,128)} %reshape.248), calls=%async_computation.2 | async-start | bytes 131072 | tf_op jit(solution)/shard_map/all_to_all | solution.py:31
  222.2 13.8 %all-to-all-start.4 = ((f32[32,1,32]{2,1,0:T(1,128)}), f32[32,1,32]{2,1,0:T(1,128)S(1)}, u32[]{:S(2)}, u32[]{:S(2)}) async-start(f32[32,1,32]{2,1,0:T(1,128)} %broadcast_in_dim.72), calls=%async_computation.5 | async-start | bytes 32768 | tf_op jit(solution)/shard_map/all_to_all | solution.py:31
Sparse Core Ops, SparseCore 0:
  11.1 88.2 all-gather.1
  131.5 61.1 reduce-scatter.1
where the time goes:
time: 245 us
  waiting for transfers between devices  151 us (62%)
  starting transfers between devices  29 us (12%)
  matrix products  17.9 us (7%)
  other arithmetic  17.3 us (7%)
  between operations  16.2 us (7%)
  local copies, waits for them, and re-layouts  12.9 us (5%)
    all_gather x1, waiting for transfers between devices, gather_turned(): out = lax.all_gather(both, axis, axis=0, tiled=True)  89.8 us
    reduce_scatter x1, waiting for transfers between devices, shards(): lax.psum_scatter(jnp.dot(normed, head_weight, preferred_element_type=jnp....  33.1 us
    all_to_all x3, starting transfers between devices, sent_to_all(): lax.all_to_all(jnp.broadcast_to(shard[None], (devices, *shard.shape)), ax...  19.7 us
    dot_general x1, matrix products, shards(): jnp.dot(normed, head_weight, preferred_element_type=jnp.float32)  17.9 us
    all_to_all x3, waiting for transfers between devices, sent_to_all(): lax.all_to_all(jnp.broadcast_to(shard[None], (devices, *shard.shape)), ax...  16.7 us
    all_to_all x2, waiting for transfers between devices, exchange_in_order(): out = lax.all_to_all(out, axes[k], k, k, tiled=True)  11.8 us
    all_to_all x2, starting transfers between devices, exchange_in_order(): out = lax.all_to_all(out, axes[k], k, k, tiled=True)  9.18 us
  transfers between devices with their start and end apart: 7, of which 6 were waited for; matrix products, arithmetic and copies ran while one was open for 6% of the time, Pallas kernels for 0%

commit v1 on v0

--- a/solution.py
+++ b/solution.py
@@ -16,7 +16,8 @@
     turned = [jnp.moveaxis(a, dim, 0) for a, dim in zip(arrays, dims)]
     widths = [t[0].size for t in turned]
     both = jnp.concatenate([t.reshape(-1, w) for t, w in zip(turned, widths)], axis=1)
-    out = lax.all_gather(both, axis, axis=0, tiled=True)
+    sent = jnp.stack([both] * lax.axis_size(axis))
+    out = jnp.concatenate(lax.all_to_all(sent, axis, 0, 0), axis=0)
     tiles = jnp.split(out, [sum(widths[:k]) for k in range(1, len(widths))], axis=1)
     return tuple(
         (

time: 245 us -> 295 us (1.20)
  blocking collectives: 0 us -> 141 us
  waiting for transfers between devices: 151 us -> 61.2 us
  local copies, waits for them, and re-layouts: 12.9 us -> 16.1 us
  other arithmetic: 17.3 us -> 14.2 us
    all_to_all x0 -> x1, blocking collectives: none -> 141 us  [gather_turned(): out = jnp.concatenate(lax.all_to_all(sent, axis, 0, 0), axis=0)]
    all_gather x1 -> x0, waiting for transfers between devices: 89.8 us -> none  [gather_turned(): out = lax.all_gather(both, axis, axis=0, tiled=True)]
  transfers between devices with their start and end apart: 7 -> 6, of which waited for: 6 -> 5; matrix products, arithmetic and copies ran while one was open for 6% -> 5% of each run, Pallas kernels for 0% -> 0%
where the time goes in v1:
time: 295 us; the launch traced here: 294 us
  blocking collectives  141 us (48%)
  waiting for transfers between devices  61.2 us (21%)
  starting transfers between devices  28.2 us (10%)
  matrix products  17.9 us (6%)
  between operations  16.2 us (5%)
  local copies, waits for them, and re-layouts  16.1 us (5%)
  other arithmetic  14.2 us (5%)
    all_to_all x1, blocking collectives, gather_turned(): out = jnp.concatenate(lax.all_to_all(sent, axis, 0, 0), axis=0)  141 us
    reduce_scatter x1, waiting for transfers between devices, shards(): lax.psum_scatter(jnp.dot(normed, head_weight, preferred_element_type=jnp....  32.6 us
    all_to_all x3, starting transfers between devices, sent_to_all(): lax.all_to_all(jnp.broadcast_to(shard[None], (devices, *shard.shape)), ax...  19.9 us
    dot_general x1, matrix products, shards(): jnp.dot(normed, head_weight, preferred_element_type=jnp.float32)  17.9 us
    all_to_all x3, waiting for transfers between devices, sent_to_all(): lax.all_to_all(jnp.broadcast_to(shard[None], (devices, *shard.shape)), ax...  16.7 us
    all_to_all x2, waiting for transfers between devices, exchange_in_order(): out = lax.all_to_all(out, axes[k], k, k, tiled=True)  12 us
    all_to_all x2, starting transfers between devices, exchange_in_order(): out = lax.all_to_all(out, axes[k], k, k, tiled=True)  8.21 us
  transfers between devices with their start and end apart: 6, of which 5 were waited for; matrix products, arithmetic and copies ran while one was open for 5% of the time, Pallas kernels for 0%

profile of v1, /device:TPU:2, one launch (start us, length us, event | category | flops | bytes accessed | tf_op | source)
XLA Modules:
  0.0 294.4 jit_solution(1211645814927416341)
XLA Ops:
  7.2 0.8 copy.46
  7.9 0.9 pad_maximum_fusion
  8.9 0.7 stack.2
  9.6 140.6 %all_to_all.32 = bf16[32,64,1281]{2,1,0:T(8,128)(2,1)S(1)} all-to-all(bf16[32,64,1281]{2,1,0:T(8,128)(2,1)S(1)} %stack.2), channel_id=1, replica_groups=mesh['dp'=8,'tensor_0'=8,'tensor_1'=4] {'tensor_0','tensor_1'}, dimensions={0} | all-to-all | bytes 10493952 | tf_op jit(solution)/shard_map/all_to_all | solution.py:20
  150.2 2.5 copy-done
  152.6 1.1 fusion
  154.4 4.5 %all-to-all-start.1 = ((f32[8,1,1280]{2,1,0:T(1,128)}), f32[8,1,1280]{2,1,0:T(1,128)S(1)}, u32[]{:S(2)}, u32[]{:S(2)}) async-start(f32[8,1,1280]{2,1,0:T(1,128)} %broadcast_in_dim.59), calls=%async_computation.1 | async-start | bytes 81920 | tf_op jit(solution)/shard_map/all_to_all | solution.py:32
  158.9 1.3 convert_reduce_fusion
  160.2 4.2 %all-to-all-done.1 = f32[8,1,1280]{2,1,0:T(1,128)S(1)} async-done(((f32[8,1,1280]{2,1,0:T(1,128)}), f32[8,1,1280]{2,1,0:T(1,128)S(1)}, u32[]{:S(2)}, u32[]{:S(2)}) %all-to-all-start.1) | async-done | bytes 40992 | tf_op jit(solution)/shard_map/all_to_all | solution.py:32
  164.4 17.9 %fusion.3 = f32[1280,2048]{1,0:T(8,128)} fusion(bf16[2048,2048]{1,0:T(8,128)(2,1)} %param.8, f32[2048]{0:T(1024)S(1)} %convert_reduce_fusion, f32[1280]{0:T(1024)S(1)} %add_rsqrt_fusion, bf16[2048,1281]{1,0:T(8,128)(2,1)} %bitcast.29), kind=kOutput, calls=%fused_computation.7 | convolution fusion | flops 10747904000 | bytes 24130560 | tf_op jit(solution)/shard_map/dot_general | solution.py:110
  185.5 2.4 fusion.8
  187.9 0.8 select_n.68
  188.7 3.4 %all-to-all-start.3 = ((f32[8,4,1,2048]{3,1,2,0:T(4,128)}), f32[8,4,1,2048]{3,1,2,0:T(4,128)S(1)}, u32[]{:S(2)}, u32[]{:S(2)}) async-start(f32[8,4,1,2048]{3,1,2,0:T(4,128)} %select_n.68), calls=%async_computation.4 | async-start | bytes 524288 | tf_op jit(solution)/shard_map/all_to_all | solution.py:87
  192.1 12.0 %all-to-all-done.3 = f32[8,4,1,2048]{3,1,2,0:T(4,128)S(1)} async-done(((f32[8,4,1,2048]{3,1,2,0:T(4,128)}), f32[8,4,1,2048]{3,1,2,0:T(4,128)S(1)}, u32[]{:S(2)}, u32[]{:S(2)}) %all-to-all-start.3) | async-done | bytes 262176 | tf_op jit(solution)/shard_map/all_to_all | solution.py:87
  204.1 0.9 copy.51
  205.0 4.8 %all-to-all-start.4 = ((f32[8,4,1,2048]{3,0,2,1:T(8,128)}), f32[8,4,1,2048]{3,0,2,1:T(8,128)S(1)}, u32[]{:S(2)}, u32[]{:S(2)}) async-start(f32[8,4,1,2048]{3,0,2,1:T(8,128)} %copy.51), calls=%async_computation.5 | async-start | bytes 524288 | tf_op jit(solution)/shard_map/all_to_all | solution.py:87
  209.8 32.6 %reduce-scatter.2.cloned.1.call-done = f32[160,2048]{1,0:T(8,128)} async-done(((f32[1280,2048]{1,0:T(8,128)}), f32[160,2048]{1,0:T(8,128)}) %reduce-scatter.2.cloned.1.call-update) | async-done | bytes 1310736 | tf_op jit(solution)/shard_map/reduce_scatter | solution.py:109
  242.3 1.5 reduce_max.9
  243.8 1.8 exponential_reduce_fusion
  245.6 0.8 reshape.254
  246.5 10.2 %all-to-all-start.2 = ((f32[32,1,480]{2,1,0:T(1,128)}), f32[32,1,480]{2,1,0:T(1,128)S(1)}, u32[]{:S(2)}, u32[]{:S(2)}) async-start(f32[32,1,480]{2,1,0:T(1,128)} %reshape.254), calls=%async_computation.3 | async-start | bytes 131072 | tf_op jit(solution)/shard_map/all_to_all | solution.py:32
  256.8 0.8 reshape_reshape.3
  257.6 1.5 reshape.182
  259.1 0.8 copy.50
  259.8 0.9 gather_fusion
  260.8 4.5 %all-to-all-done.2 = f32[32,1,480]{2,1,0:T(1,128)S(1)} async-done(((f32[32,1,480]{2,1,0:T(1,128)}), f32[32,1,480]{2,1,0:T(1,128)S(1)}, u32[]{:S(2)}, u32[]{:S(2)}) %all-to-all-start.2) | async-done | bytes 61472 | tf_op jit(solution)/shard_map/all_to_all | solution.py:32
  265.8 0.8 reduce.15
  268.8 0.7 gather_fusion.1
  269.8 1.2 fusion.13
  271.9 5.3 %all-to-all-start.5 = ((f32[32,1,32]{2,1,0:T(1,128)}), f32[32,1,32]{2,1,0:T(1,128)S(1)}, u32[]{:S(2)}, u32[]{:S(2)}) async-start(f32[32,1,32]{2,1,0:T(1,128)} %broadcast_in_dim.72), calls=%async_computation.6 | async-start | bytes 32768 | tf_op jit(solution)/shard_map/all_to_all | solution.py:32
  277.7 8.0 %all-to-all-done.5 = f32[32,1,32]{2,1,0:T(1,128)S(1)} async-done(((f32[32,1,32]{2,1,0:T(1,128)}), f32[32,1,32]{2,1,0:T(1,128)S(1)}, u32[]{:S(2)}, u32[]{:S(2)}) %all-to-all-start.5) | async-done | bytes 4128 | tf_op jit(solution)/shard_map/all_to_all | solution.py:32
  285.7 1.8 multiply_divide_fusion
  (73 shorter events, 6.5 us)
Async XLA Ops:
  150.2 2.5 copy-start
  154.4 10.0 %all-to-all-start.1 = ((f32[8,1,1280]{2,1,0:T(1,128)}), f32[8,1,1280]{2,1,0:T(1,128)S(1)}, u32[]{:S(2)}, u32[]{:S(2)}) async-start(f32[8,1,1280]{2,1,0:T(1,128)} %broadcast_in_dim.59), calls=%async_computation.1 | async-start | bytes 81920 | tf_op jit(solution)/shard_map/all_to_all | solution.py:32
  158.9 83.5 %reduce-scatter.2.cloned.1.call-start = ((), (), s32[]{:S(2)}) async-start(), calls=%async_computation.7 | async-start | bytes 11796480 | tf_op jit(solution)/shard_map/reduce_scatter | solution.py:109
  182.3 0.7 copy-start.3
  182.3 61.5 %copy-start.2 = (s32[160]{0:T(256)S(1)}, s32[160]{0:T(256)}, u32[]{:S(2)}) copy-start(s32[160]{0:T(256)} %param.10) | copy-start | bytes 1924
  188.7 15.4 %all-to-all-start.3 = ((f32[8,4,1,2048]{3,1,2,0:T(4,128)}), f32[8,4,1,2048]{3,1,2,0:T(4,128)S(1)}, u32[]{:S(2)}, u32[]{:S(2)}) async-start(f32[8,4,1,2048]{3,1,2,0:T(4,128)} %select_n.68), calls=%async_computation.4 | async-start | bytes 524288 | tf_op jit(solution)/shard_map/all_to_all | solution.py:87
  205.0 41.5 %all-to-all-start.4 = ((f32[8,4,1,2048]{3,0,2,1:T(8,128)}), f32[8,4,1,2048]{3,0,2,1:T(8,128)S(1)}, u32[]{:S(2)}, u32[]{:S(2)}) async-start(f32[8,4,1,2048]{3,0,2,1:T(8,128)} %copy.51), calls=%async_computation.5 | async-start | bytes 524288 | tf_op jit(solution)/shard_map/all_to_all | solution.py:87
  246.5 10.4 %copy-start.1 = (f32[8,4,1,2048]{3,0,2,1:T(8,128)}, f32[8,4,1,2048]{3,0,2,1:T(8,128)S(1)}, u32[]{:S(2)}) copy-start(f32[8,4,1,2048]{3,0,2,1:T(8,128)S(1)} %all-to-all-done.4) | copy-start | bytes 786436
  246.5 18.9 %all-to-all-start.2 = ((f32[32,1,480]{2,1,0:T(1,128)}), f32[32,1,480]{2,1,0:T(1,128)S(1)}, u32[]{:S(2)}, u32[]{:S(2)}) async-start(f32[32,1,480]{2,1,0:T(1,128)} %reshape.254), calls=%async_computation.3 | async-start | bytes 131072 | tf_op jit(solution)/shard_map/all_to_all | solution.py:32
  271.9 13.8 %all-to-all-start.5 = ((f32[32,1,32]{2,1,0:T(1,128)}), f32[32,1,32]{2,1,0:T(1,128)S(1)}, u32[]{:S(2)}, u32[]{:S(2)}) async-start(f32[32,1,32]{2,1,0:T(1,128)} %broadcast_in_dim.72), calls=%async_computation.6 | async-start | bytes 32768 | tf_op jit(solution)/shard_map/all_to_all | solution.py:32
Sparse Core Ops, SparseCore 0:
  182.4 59.8 reduce-scatter.1
